TPU v7x, 128 devices: a whole 4x4x4 slice. The times are simulated.
128 devices in a mesh: rep: 4 (over x), rows: 32 (over z, y, core).
Axes of the slice: x: 4, y: 4, z: 4, core: 2. Of those that a mesh axis runs over, the one named last changes fastest.
Arguments:
- node_feat: bfloat16 [131072, 50], P(('rows', 'rep'))
- degree: int32 [131072], P(('rows', 'rep'))
- nbr_col: int32 [131072, 32], P('rows', 'rep')
- nbr_wt: bfloat16 [131072, 32], P('rows', 'rep')
- nbr_mask: int32 [131072, 32], P('rows', 'rep')
- w_one: bfloat16 [50, 2048], replicated
- w_two: bfloat16 [2048, 2048], replicated
- w_three: bfloat16 [2048, 121], replicated
Outputs:
- output: float32 [131072, 121], P(('rows', 'rep'))
All inputs are finite; a program needn't handle non-finite values.
Results may differ from a plain program's by a relative error of at most 0.001.
Values are sent between devices in bfloat16 or wider.
A program may use at most 1 GiB of HBM per device.

v0:
```python
import jax
import jax.numpy as jnp
from jax import lax
from jax.sharding import PartitionSpec as P


def solution(mesh):
    rep_size = mesh.shape['rep']

    def device_body(node_feat, degree, nbr_col, nbr_wt, nbr_mask, w_one, w_two, w_three):
        node_dev = node_feat.shape[0]
        inv_sqrt = lax.rsqrt(degree.astype(jnp.float32))[:, None]
        local_idx = (nbr_col // (rep_size * node_dev)) * node_dev + nbr_col % node_dev
        edge_wt = jnp.where(nbr_mask > 0, nbr_wt, jnp.zeros_like(nbr_wt))

        def gcn_layer(hidden, w_mat):
            src_rows = (jnp.dot(hidden, w_mat, preferred_element_type=jnp.float32) * inv_sqrt).astype(jnp.bfloat16)
            range_rows = lax.all_gather(src_rows, 'rows', axis=0, tiled=True)
            picked = jnp.take(range_rows, local_idx, axis=0)
            part_sum = jnp.einsum('nk,nkf->nf', edge_wt, picked, preferred_element_type=jnp.float32)
            neigh_sum = lax.psum_scatter(part_sum, 'rep', scatter_dimension=0, tiled=True)
            return inv_sqrt * (neigh_sum + src_rows.astype(jnp.float32))

        h_one = jnp.maximum(gcn_layer(node_feat, w_one), 0.0).astype(jnp.bfloat16)
        h_two = jnp.maximum(gcn_layer(h_one, w_two), 0.0).astype(jnp.bfloat16)
        return gcn_layer(h_two, w_three)

    row_spec = P(('rows', 'rep'), None)
    table_spec = P('rows', 'rep')
    full_spec = P(None, None)
    return jax.shard_map(device_body, mesh=mesh, in_specs=(row_spec, P(('rows', 'rep')), table_spec, table_spec, table_spec, full_spec, full_spec, full_spec), out_specs=row_spec, check_vma=False)
```

profile of v0, /device:TPU:1, one launch (start us, length us, event | category | flops | bytes accessed | tf_op | source)
XLA Modules:
  0.0 3285.5 jit_solution(16308634688197117433)
XLA Ops:
  6.6 0.8 convert_rsqrt_fusion
  7.3 4.3 multiply_convert_fusion.1
  11.9 1.4 copy.12
  13.4 3.8 copy.18
  17.2 0.6 copy.15
  17.8 1.0 reshape.41
  18.8 372.4 %all-gather.4.cloned.1.call-done = bf16[32768,2048]{1,0:T(8,128)(2,1)} async-done(((bf16[1024,2048]{1,0:T(8,128)(2,1)}), bf16[32768,2048]{1,0:T(8,128)(2,1)}) %all-gather.4.cloned.1.call-update) | async-done | bytes 134217744 | tf_op jit(solution)/shard_map/all_gather | solution.py:18
  391.2 762.9 %gather_fusion.1 = bf16[32768,2048]{1,0:T(8,128)(2,1)} fusion(bf16[32768,2048]{1,0:T(8,128)(2,1)} %all-gather.4.cloned.1.call-done, s32[32768]{0:T(1024)S(1)} %broadcast_clamp_fusion), kind=kCustom, calls=%fused_computation.clone | custom fusion | bytes 268566528 | tf_op jit(solution)/shard_map/jit(_take)/gather | solution.py:19
  1154.1 63.7 %fusion.1 = f32[4096,1,2048]{2,1,0:T(1,128)} fusion(bf16[4096,8,1]{1,2,0:T(2,128)(2,1)S(1)} %copy-done.2, bf16[32768,2048]{1,0:T(8,128)(2,1)} %gather_fusion.1, pred[4096,8]{1,0:T(8,128)(4,1)S(1)} %copy-done.4), kind=kOutput, calls=%fused_computation.6 | convolution fusion | flops 201326592 | bytes 167870464 | tf_op jit(solution)/shard_map/nk,nkf->nf/dot_general | solution.py:20
  1217.8 29.8 copy.25
  1247.9 280.9 %reduce-scatter.4.cloned.1.call-done = f32[1024,2048]{1,0:T(8,128)} async-done(((f32[4096,2048]{1,0:T(8,128)}), f32[1024,2048]{1,0:T(8,128)}) %reduce-scatter.4.cloned.1.call-update) | async-done | bytes 8388624 | tf_op jit(solution)/shard_map/reduce_scatter | solution.py:21
  1528.8 15.9 multiply_convert_fusion
  1544.7 376.3 %all-gather.6.cloned.1.call-done = bf16[32768,2048]{1,0:T(8,128)(2,1)} async-done(((bf16[1024,2048]{1,0:T(8,128)(2,1)}), bf16[32768,2048]{1,0:T(8,128)(2,1)}) %all-gather.6.cloned.1.call-update) | async-done | bytes 134217744 | tf_op jit(solution)/shard_map/all_gather | solution.py:18
  1921.0 762.4 %gather_fusion.2 = bf16[32768,2048]{1,0:T(8,128)(2,1)} fusion(bf16[32768,2048]{1,0:T(8,128)(2,1)} %all-gather.6.cloned.1.call-done, s32[32768]{0:T(1024)S(1)} %broadcast_clamp_fusion), kind=kCustom, calls=%fused_computation.1.clone | custom fusion | bytes 268566528 | tf_op jit(solution)/shard_map/jit(_take)/gather | solution.py:19
  2683.4 63.7 %fusion = f32[4096,1,2048]{2,1,0:T(1,128)} fusion(bf16[4096,8,1]{1,2,0:T(2,128)(2,1)S(1)} %copy-done.3, bf16[32768,2048]{1,0:T(8,128)(2,1)} %gather_fusion.2, pred[4096,8]{1,0:T(8,128)(4,1)S(1)} %copy-done.5), kind=kOutput, calls=%fused_computation.4 | convolution fusion | flops 201326592 | bytes 167870464 | tf_op jit(solution)/shard_map/nk,nkf->nf/dot_general | solution.py:20
  2747.1 29.8 copy.24
  2777.0 281.1 %reduce-scatter.6.cloned.1.call-done = f32[1024,2048]{1,0:T(8,128)} async-done(((f32[4096,2048]{1,0:T(8,128)}), f32[1024,2048]{1,0:T(8,128)}) %reduce-scatter.6.cloned.1.call-update) | async-done | bytes 8388624 | tf_op jit(solution)/shard_map/reduce_scatter | solution.py:21
  3058.1 6.7 fusion.13
  3064.8 0.3 reduce-scatter.8.cloned.1.call-start
  3065.1 52.9 %all-gather.8.cloned.1.call-done = bf16[32768,121]{1,0:T(8,128)(2,1)} async-done(((bf16[1024,121]{1,0:T(8,128)(2,1)}), bf16[32768,121]{1,0:T(8,128)(2,1)}) %all-gather.8.cloned.1.call-update) | async-done | bytes 7929872 | tf_op jit(solution)/shard_map/all_gather | solution.py:18
  3118.0 114.7 %gather_fusion = bf16[32768,121]{1,0:T(8,128)(2,1)} fusion(bf16[32768,121]{1,0:T(8,128)(2,1)} %all-gather.8.cloned.1.call-done, s32[32768]{0:T(1024)S(1)} %broadcast_clamp_fusion), kind=kCustom, calls=%fused_computation.2 | custom fusion | bytes 15990784 | tf_op jit(solution)/shard_map/jit(_take)/gather | solution.py:19
  3232.7 15.3 fusion.6
  3248.0 28.6 reduce-scatter.8.cloned.1.call-done
  3276.6 2.0 add_multiply_fusion
  (38 shorter events, 0.7 us)
Async XLA Ops:
  6.5 3051.5 %copy-start = (bf16[2048,121]{1,0:T(8,128)(2,1)S(1)}, bf16[2048,121]{1,0:T(8,128)(2,1)}, u32[]{:S(2)}) copy-start(bf16[2048,121]{1,0:T(8,128)(2,1)} %param.17) | copy-start | bytes 1486852
  6.5 5.2 copy-start.6
  6.5 6.8 copy-start.7
  6.5 6.8 copy-start.8
  6.5 384.7 %all-gather.4.cloned.1.call-start = ((), (), s32[]{:S(2)}) async-start(), calls=%async_computation.3 | async-start | bytes 138412032 | tf_op jit(solution)/shard_map/all_gather | solution.py:18
  7.3 4.3 copy-start.9
  11.7 1517.1 %reduce-scatter.4.cloned.1.call-start = ((), (), s32[]{:S(2)}) async-start(), calls=%async_computation.4 | async-start | bytes 41943040 | tf_op jit(solution)/shard_map/reduce_scatter | solution.py:21
  391.2 762.9 %copy-start.2 = (bf16[4096,8,1]{1,2,0:T(2,128)(2,1)S(1)}, bf16[4096,8,1]{1,2,0:T(2,128)(2,1)}, u32[]{:S(2)}) copy-start(bf16[4096,8,1]{1,2,0:T(2,128)(2,1)} %copy.18) | copy-start | bytes 196612
  391.2 762.9 %copy-start.4 = (pred[4096,8]{1,0:T(8,128)(4,1)S(1)}, pred[4096,8]{1,0:T(8,128)(4,1)}, u32[]{:S(2)}) copy-start(pred[4096,8]{1,0:T(8,128)(4,1)} %copy.12) | copy-start | bytes 98308
  1247.7 281.1 %copy-start.10 = (f32[1024]{0:T(1024)S(1)}, f32[1024]{0:T(1024)}, u32[]{:S(2)}) copy-start(f32[1024]{0:T(1024)} %copy-done.9) | copy-start | bytes 12292
  1247.7 673.3 %all-gather.6.cloned.1.call-start = ((), (), s32[]{:S(2)}) async-start(), calls=%async_computation.5 | async-start | bytes 138412032 | tf_op jit(solution)/shard_map/all_gather | solution.py:18
  1544.7 1513.4 %reduce-scatter.6.cloned.1.call-start = ((), (), s32[]{:S(2)}) async-start(), calls=%async_computation.6 | async-start | bytes 41943040 | tf_op jit(solution)/shard_map/reduce_scatter | solution.py:21
  1921.0 762.4 %copy-start.3 = (bf16[4096,8,1]{1,2,0:T(2,128)(2,1)S(1)}, bf16[4096,8,1]{1,2,0:T(2,128)(2,1)}, u32[]{:S(2)}) copy-start(bf16[4096,8,1]{1,2,0:T(2,128)(2,1)} %copy.18) | copy-start | bytes 196612
  1921.0 762.4 %copy-start.5 = (pred[4096,8]{1,0:T(8,128)(4,1)S(1)}, pred[4096,8]{1,0:T(8,128)(4,1)}, u32[]{:S(2)}) copy-start(pred[4096,8]{1,0:T(8,128)(4,1)} %copy.12) | copy-start | bytes 98308
  2776.9 281.1 %copy-start.11 = (f32[1024]{0:T(1024)S(1)}, f32[1024]{0:T(1024)}, u32[]{:S(2)}) copy-start(f32[1024]{0:T(1024)} %copy-done.9) | copy-start | bytes 12292
  2777.0 341.1 %all-gather.8.cloned.1.call-start = ((), (), s32[]{:S(2)}) async-start(), calls=%async_computation.7 | async-start | bytes 8650752 | tf_op jit(solution)/shard_map/all_gather | solution.py:18
  3064.8 211.8 %reduce-scatter.8.cloned.1.call-start = ((), (), s32[]{:S(2)}) async-start(), calls=%async_computation.8 | async-start | bytes 2621440 | tf_op jit(solution)/shard_map/reduce_scatter | solution.py:21
  3232.7 44.0 %copy-start.1 = (bf16[1024,121]{1,0:T(8,128)(2,1)S(1)}, bf16[1024,121]{1,0:T(8,128)(2,1)}, u32[]{:S(2)}) copy-start(bf16[1024,121]{1,0:T(8,128)(2,1)} %fusion.13) | copy-start | bytes 743428
Sparse Core Ops, SparseCore 0:
  11.8 379.3 all-gather.3
  1247.8 280.9 reduce-scatter.3
  1544.8 376.1 all-gather.5
  2777.1 280.9 reduce-scatter.5
  3065.0 53.0 all-gather.7
  3248.2 28.4 reduce-scatter.7
where the time goes:
time: 3320 us; the launch traced here: 3290 us
  local copies, waits for them, and re-layouts  1710 us (52%)
  waiting for transfers between devices  1390 us (42%)
  matrix products  170 us (5%)
    gather x3, local copies, waits for them, and re-layouts, gcn_layer(): picked = jnp.take(range_rows, local_idx, axis=0)  1640 us
    all_gather x3, waiting for transfers between devices, gcn_layer(): range_rows = lax.all_gather(src_rows, 'rows', axis=0, tiled=True)  802 us
    reduce_scatter x3, waiting for transfers between devices, gcn_layer(): lax.psum_scatter(part_sum, 'rep', scatter_dimension=0, tiled=True)  591 us
    dot_general x3, matrix products, gcn_layer(): jnp.einsum('nk,nkf->nf', edge_wt, picked, preferred_element_type=jnp.floa...  143 us
  transfers between devices with their start and end apart: 6, of which 6 were waited for; matrix products, arithmetic and copies ran while one was open for 0% of the time, Pallas kernels for 0%

commit v1 on v0

v1 whole, which is shorter than its diff:
```python
import functools

import jax
import jax.numpy as jnp
from jax import lax
from jax.experimental import pallas as pl
from jax.experimental.pallas import tpu as pltpu
from jax.sharding import Mesh, PartitionSpec as P

LANES = 128
PAD = 8
GROUP = 1024
BUFS = 4


def gather_kernel(meta_ref, idx_hbm, wt_ref, src_hbm, *refs, phases, groups, blocked, from_feat, swap_core, finish):
    if from_feat:
        wbd_ref, deg_ref, out_ref, table, acc, stage, *rest = refs
    else:
        out_ref, table, acc, stage, *rest = refs
    sbufs, (sem_idx, sem_stage) = rest[:BUFS], rest[BUFS:]
    total = phases * groups
    n_blk = 32
    blk_rows = stage.shape[1]

    def stage_copy(p, b):
        src_b = (b % 16) * 2 + b // 16 if swap_core else b
        return pltpu.make_async_copy(src_hbm.at[p, src_b], stage.at[b], sem_stage.at[b])

    def idx_start(q):
        if blocked:
            p, gi = q // groups, q % groups
            return (((gi // 8) * phases + p) * 8 + gi % 8) * GROUP
        return q * GROUP

    def wt_index(p, gi):
        if blocked:
            return ((gi // 8) * (phases + 1) + p) * 8 + gi % 8
        return gi

    def idx_copy(q, b):
        return pltpu.make_async_copy(idx_hbm.at[pl.ds(pl.multiple_of(idx_start(q), GROUP), GROUP)], sbufs[b], sem_idx.at[b])

    for b in range(BUFS):
        idx_copy(b, b).start()

    def start_stage(p):
        def one(b, c):
            stage_copy(p, b).start()
            return c
        lax.fori_loop(0, n_blk, one, 0)

    start_stage(0)
    sub = lax.broadcasted_iota(jnp.int32, (8, LANES), 0)
    masks = [sub == j for j in range(8)]

    def zero(t, c):
        acc[pl.ds(pl.multiple_of(t * LANES, LANES), LANES), :] = jnp.zeros((LANES, LANES), jnp.float32)
        return c
    lax.fori_loop(0, acc.shape[0] // LANES, zero, 0)

    def phase(p, carry):
        def build(b, c):
            stage_copy(p, b).wait()
            r0 = pl.multiple_of(PAD + b * 1024, 8)
            if from_feat:
                x = stage[b]
                h = jnp.dot(x, wbd_ref[...], preferred_element_type=jnp.float32)
                d = jnp.dot(x, deg_ref[...], preferred_element_type=jnp.float32)
                v = (h * lax.rsqrt(d)).astype(jnp.bfloat16).astype(jnp.float32)
                table[pl.ds(r0, 512), :] = v[:, :LANES]
                table[pl.ds(r0 + 512, 512), :] = v[:, LANES:]
            else:
                table[pl.ds(r0, 1024), :] = stage[b].astype(jnp.float32)
            return c
        lax.fori_loop(0, n_blk, build, 0)

        @pl.when(p + 1 < phases)
        def _():
            start_stage(p + 1)

        def quad(t, c):
            for b in range(BUFS):
                gi = t * BUFS + b
                q = p * groups + gi
                idx_copy(q, b).wait()
                sref = sbufs[b]
                w = wt_ref[wt_index(p, gi)].astype(jnp.float32)
                for o in range(16):
                    a = None
                    for k in range(8):
                        m = None
                        for j in range(8):
                            v = table[pl.ds(sref[o * 64 + k * 8 + j], 8), :]
                            m = v if m is None else jnp.where(masks[j], v, m)
                        e = m * jnp.broadcast_to(w[:, o * 8 + k:o * 8 + k + 1], (8, LANES))
                        a = e if a is None else a + e
                    r = pl.multiple_of(gi * 128 + o * 8, 8)
                    acc[pl.ds(r, 8), :] += a

                @pl.when(q + BUFS < total)
                def _():
                    idx_copy(q + BUFS, b).start()
            return c
        lax.fori_loop(0, groups // BUFS, quad, 0)

        if finish:
            @pl.when(p == meta_ref[0])
            def _():
                def own(t, c):
                    r = pl.multiple_of(t * LANES, LANES)
                    o = pl.multiple_of(PAD + meta_ref[1] * (groups * LANES) + r, 8)
                    acc[pl.ds(r, LANES), :] += table[pl.ds(o, LANES), :]
                    return c
                lax.fori_loop(0, groups, own, 0)
        return carry
    lax.fori_loop(0, phases, phase, 0)

    if finish:
        def close(gi, c):
            s = lax.rsqrt(wt_ref[wt_index(phases, gi)].astype(jnp.float32))
            for o in range(0, 16, 2):
                r = pl.multiple_of(gi * 128 + o * 8, 16)
                sb = jnp.concatenate([jnp.broadcast_to(s[:, o + t:o + t + 1], (8, LANES)) for t in range(2)], axis=0)
                out_ref[pl.ds(r, 16), :] = jnp.maximum(acc[pl.ds(r, 16), :] * sb, 0.0).astype(jnp.bfloat16)
            return c
        lax.fori_loop(0, groups, close, 0)
    else:
        def close(t, c):
            r = pl.multiple_of(t * LANES, LANES)
            out_ref[pl.ds(r, LANES), :] = acc[pl.ds(r, LANES), :]
            return c
        lax.fori_loop(0, groups, close, 0)


def gather_call(meta, idx, wt, src, extra=(), *, phases, groups, blocked, from_feat, swap_core, finish, name):
    vm = pl.BlockSpec(memory_space=pltpu.VMEM)
    hb = pl.BlockSpec(memory_space=pl.ANY)
    rows = groups * LANES
    blk = src.shape[2]
    kern = functools.partial(gather_kernel, phases=phases, groups=groups, blocked=blocked, from_feat=from_feat, swap_core=swap_core, finish=finish)
    return pl.pallas_call(
        kern,
        out_shape=jax.ShapeDtypeStruct((rows, LANES), jnp.bfloat16 if finish else jnp.float32),
        in_specs=[pl.BlockSpec(memory_space=pltpu.SMEM), hb, vm, hb] + [vm] * len(extra),
        out_specs=vm,
        scratch_shapes=[
            pltpu.VMEM((PAD + 32768 + 8, LANES), jnp.float32),
            pltpu.VMEM((rows, LANES), jnp.float32),
            pltpu.VMEM((32, blk, LANES), jnp.bfloat16),
            *[pltpu.SMEM((GROUP,), jnp.int32) for _ in range(BUFS)],
            pltpu.SemaphoreType.DMA((BUFS,)),
            pltpu.SemaphoreType.DMA((32,)),
        ],
        compiler_params=pltpu.CompilerParams(vmem_limit_bytes=60 * 2**20),
        cost_estimate=pl.CostEstimate(flops=phases * groups * 2000000, bytes_accessed=2**25, transcendentals=0),
        name=name,
    )(meta, idx, wt, src, *extra)


def solution(mesh):
    mesh4 = Mesh(mesh.devices.reshape(4, 4, 4, 2), ('rep', 'z', 'y', 'core'))

    def device_body(node_feat, degree, nbr_col, nbr_wt, nbr_mask, w_one, w_two, w_three):
        bf = jnp.bfloat16
        nodes, f_in = node_feat.shape
        hid, cls = w_three.shape
        rep, core = lax.axis_index('rep'), lax.axis_index('core')
        fgroup = lax.axis_index('z') * 4 + lax.axis_index('y')
        inv_sqrt = lax.rsqrt(degree.astype(jnp.float32))[:, None]
        meta = jnp.stack([rep, core]).astype(jnp.int32)

        half = jnp.concatenate([node_feat, degree.astype(bf)[:, None], jnp.zeros((nodes, 64 - f_in - 1), bf)], axis=1)
        packed = jnp.concatenate([half[:nodes // 2], half[nodes // 2:]], axis=1)
        feats = lax.all_gather(packed, ('rep', 'z', 'y', 'core'), axis=0).reshape(4, 32, nodes // 2, LANES)

        blk = nbr_col // (4 * nodes)
        pos = ((blk % 2) * 16 + blk // 2) * nodes + nbr_col % nodes
        pos = pos + PAD - (jnp.arange(4 * nodes) % 8)[:, None]
        idx_own = pos.reshape(-1, 8, 8).transpose(0, 2, 1).reshape(-1)
        edge_wt = jnp.where(nbr_mask > 0, nbr_wt, jnp.zeros_like(nbr_wt))
        wt_own = edge_wt.reshape(-1, 16, 8, 8).transpose(0, 2, 1, 3).reshape(-1, 8, LANES)
        idx_all = lax.all_gather(lax.all_to_all(idx_own.reshape(4, -1), 'rep', 0, 0), ('z', 'y'), axis=0).reshape(-1)
        deg_own = degree.astype(bf).reshape(1, -1, 16, 8).transpose(0, 1, 3, 2)
        deg_own = jnp.pad(deg_own, ((0, 0), (0, 0), (0, 0), (0, LANES - 16)), constant_values=1)
        wt_mine = lax.all_to_all(wt_own.reshape(4, -1, 8, LANES), 'rep', 0, 0)
        wt_all = lax.all_gather(jnp.concatenate([wt_mine, deg_own], axis=0), ('z', 'y'), axis=0).reshape(-1, 8, LANES)

        w_loc = lax.dynamic_slice_in_dim(w_one, fgroup * LANES, LANES, axis=1)
        wbd = jnp.zeros((LANES, 2 * LANES), bf).at[:f_in, :LANES].set(w_loc).at[64:64 + f_in, LANES:].set(w_loc)
        ebd = jnp.zeros((LANES, 2 * LANES), bf).at[f_in, :LANES].set(1).at[64 + f_in, LANES:].set(1)

        def back(h):
            parts = lax.all_to_all(h.reshape(16, nodes, LANES), ('z', 'y'), 0, 0)
            return parts.transpose(1, 0, 2).reshape(nodes, hid)

        h_one = back(gather_call(meta, idx_all, wt_all, feats, (wbd, ebd), phases=4, groups=128, blocked=True, from_feat=True,
                                 swap_core=True, finish=True, name='layer_one'))
        s_two = (jnp.dot(h_one, w_two, preferred_element_type=jnp.float32) * inv_sqrt).astype(bf)
        s_two = lax.all_to_all(s_two.reshape(nodes, 16, LANES).transpose(1, 0, 2), ('z', 'y'), 0, 0)
        s_two = lax.all_gather(s_two, ('rep', 'core'), axis=0).reshape(4, 32, nodes, LANES)
        h_two = back(gather_call(meta, idx_all, wt_all, s_two, phases=4, groups=128, blocked=True, from_feat=False,
                                 swap_core=False, finish=True, name='layer_two'))
        w_pad = jnp.pad(w_three, ((0, 0), (0, LANES - cls)))
        s_three = (jnp.dot(h_two, w_pad, preferred_element_type=jnp.float32) * inv_sqrt).astype(bf)
        s_all = lax.all_gather(s_three, ('z', 'y', 'core'), axis=0).reshape(1, 32, nodes, LANES)
        part = gather_call(meta, idx_own, wt_own, s_all, phases=1, groups=32, blocked=False, from_feat=False,
                           swap_core=True, finish=False, name='layer_three')
        neigh = lax.psum_scatter(part, 'rep', scatter_dimension=0, tiled=True)
        return (inv_sqrt * (neigh + s_three.astype(jnp.float32)))[:, :cls]

    rows = ('z', 'y', 'core')
    row_spec = P((*rows, 'rep'), None)
    table_spec = P(rows, 'rep')
    full = P(None, None)
    return jax.shard_map(device_body, mesh=mesh4, in_specs=(row_spec, P((*rows, 'rep')), table_spec, table_spec, table_spec, full, full, full),
                         out_specs=row_spec, check_vma=False)
```

time: 3320 us -> 1450 us (0.44); the launches traced: 3290 us -> 1450 us
  local copies, waits for them, and re-layouts: 1710 us -> 53.4 us
  waiting for transfers between devices: 1390 us -> 424 us
  Pallas kernels: 0 us -> 803 us
  matrix products: 170 us -> 14.7 us
  blocking collectives: 0 us -> 124 us
    gather x3 -> x0, local copies, waits for them, and re-layouts: 1640 us -> none  [gcn_layer(): picked = jnp.take(range_rows, local_idx, axis=0)]
    pallas_call x0 -> x3, Pallas kernels: none -> 803 us  [gather_call(): pl.pallas_call(kern, out_shape=jax.ShapeDtypeStruct((rows, LANES), jnp.bf...]
    reduce_scatter x3 -> x1, waiting for transfers between devices: 591 us -> 28.6 us  [device_body(): neigh = lax.psum_scatter(part, 'rep', scatter_dimension=0, tiled=True)]
    all_gather x3 -> x5, waiting for transfers between devices: 802 us -> 333 us  [the longest x1 154 us: device_body(): lax.all_gather(s_two, ('rep', 'core'), axis=0).reshape(4, 32, nodes, LANES)]
    dot_general x6 -> x2, matrix products: 170 us -> 14.7 us  [the longest x1 12.7 us: device_body(): jnp.dot(h_one, w_two, preferred_element_type=jnp.float32) * inv_sqrt]
    all_to_all x0 -> x3, blocking collectives: none -> 124 us  [the longest x1 59 us: back(): parts = lax.all_to_all(h.reshape(16, nodes, LANES), ('z', 'y'), 0, 0)]
    all_to_all x0 -> x2, waiting for transfers between devices: none -> 62.8 us  [the longest x1 58.7 us: back(): parts = lax.all_to_all(h.reshape(16, nodes, LANES), ('z', 'y'), 0, 0)]
    dot_general x2 -> x0, local copies, waits for them, and re-layouts: 59.6 us -> none  [gcn_layer(): jnp.einsum('nk,nkf->nf', edge_wt, picked, preferred_element_type=jnp.floa...]
  transfers between devices with their start and end apart: 6 -> 8, of which waited for: 6 -> 8; matrix products, arithmetic and copies ran while one was open for 0% -> 3% of each run, Pallas kernels for 0% -> 0%
where the time goes in v1:
time: 1450 us
  Pallas kernels  803 us (55%)
  waiting for transfers between devices  424 us (29%)
  blocking collectives  124 us (9%)
  local copies, waits for them, and re-layouts  53.4 us (4%)
  matrix products  14.7 us (1%)
    pallas_call x3, Pallas kernels, gather_call(): pl.pallas_call(kern, out_shape=jax.ShapeDtypeStruct((rows, LANES), jnp.bf...  803 us
    all_gather x1, waiting for transfers between devices, device_body(): lax.all_gather(s_two, ('rep', 'core'), axis=0).reshape(4, 32, nodes, LANES)  154 us
    all_gather x1, waiting for transfers between devices, device_body(): lax.all_gather(packed, ('rep', 'z', 'y', 'core'), axis=0)  62.8 us
    all_to_all x1, blocking collectives, back(): parts = lax.all_to_all(h.reshape(16, nodes, LANES), ('z', 'y'), 0, 0)  59 us
    all_to_all x1, waiting for transfers between devices, back(): parts = lax.all_to_all(h.reshape(16, nodes, LANES), ('z', 'y'), 0, 0)  58.7 us
    all_to_all x1, blocking collectives, device_body(): lax.all_to_all(s_two.reshape(nodes, 16, LANES).transpose(1, 0, 2), ('z',...  57.5 us
    all_gather x1, waiting for transfers between devices, device_body(): lax.all_gather(s_three, ('z', 'y', 'core'), axis=0)  49.1 us
    all_gather x1, waiting for transfers between devices, device_body(): lax.all_gather(lax.all_to_all(idx_own.reshape(4, -1), 'rep', 0, 0), ('z',...  46.7 us
  transfers between devices with their start and end apart: 8, of which 8 were waited for; matrix products, arithmetic and copies ran while one was open for 3% of the time, Pallas kernels for 0%

profile of v1, /device:TPU:1, one launch (start us, length us, event | category | flops | bytes accessed | tf_op | source)
XLA Modules:
  0.0 1450.2 jit_solution(13509751237974868067)
XLA Ops:
  14.6 4.8 all-to-all-start.1
  19.7 4.1 all-to-all-done.1
  24.7 2.5 reshape.166
  27.2 2.8 copy.22
  31.1 7.8 all_to_all.30
  40.0 62.8 %all-gather.15.cloned.1.call-done = bf16[65536,128]{0,1:T(8,128)(2,1)} async-done(((bf16[512,128]{0,1:T(8,128)(2,1)}), bf16[65536,128]{0,1:T(8,128)(2,1)}) %all-gather.15.cloned.1.call-update) | async-done | bytes 16777232 | tf_op jit(solution)/shard_map/all_gather | solution.py:175
  102.8 22.3 %copy.28 = bf16[65536,128]{1,0:T(8,128)(2,1)} copy(bf16[65536,128]{0,1:T(8,128)(2,1)} %all-gather.15.cloned.1.call-done) | data formatting | bytes 33554432 | tf_op jit(solution)/shard_map/all_gather | solution.py:175
  125.1 20.3 %all-gather.13.cloned.1.call-done = bf16[80,8,8,128]{3,2,1,0:T(8,128)(2,1)} async-done(((bf16[5,8,8,128]{3,2,1,0:T(8,128)(2,1)}), bf16[80,8,8,128]{3,2,1,0:T(8,128)(2,1)}) %all-gather.13.cloned.1.call-update) | async-done | bytes 1310736 | tf_op jit(solution)/shard_map/all_gather | solution.py:187
  145.5 46.7 %all-gather.11.cloned.1.call-done = s32[64,1,8192]{2,1,0:T(1,128)} async-done(((s32[4,1,8192]{2,1,0:T(1,128)}), s32[64,1,8192]{2,1,0:T(1,128)}) %all-gather.11.cloned.1.call-update) | async-done | bytes 2097168 | tf_op jit(solution)/shard_map/all_gather | solution.py:183
  192.2 403.9 %layer_one.1 = bf16[16384,128]{1,0:T(8,128)(2,1)} custom-call(s32[2]{0:T(128)} %pad_add_fusion.meta_ref, s32[524288]{0:T(1024)} %bitcast.45, bf16[640,8,128]{2,1,0:T(8,128)(2,1)} %bitcast.47, bf16[4,32,512,128]{3,2,1,0:T(8,128)(2,1)} %bitcast.36, bf16[128,256]{1,0:T(8,128)(2,1)} %copy-done.3, bf16[128,256]{1,0:T(8,128)(2,1)} %constant.211.clone.1.refs_1_), custom_call_target="tpu_custom_call" | custom-call | flops 1024000000 | bytes 33554432 | tf_op jit(solution)/shard_map/layer_one/pallas_call | solution.py:142
  596.1 6.5 copy.29
  602.6 4.9 all-to-all-start.2
  607.7 58.7 %all-to-all-done.2 = bf16[16,1024,128]{1,2,0:T(8,128)(2,1)} async-done(((bf16[16,1024,128]{1,2,0:T(8,128)(2,1)}), bf16[16,1024,128]{1,2,0:T(8,128)(2,1)}, u32[]{:S(2)}, u32[]{:S(2)}) %all-to-all-start.2) | async-done | bytes 4194336 | tf_op jit(solution)/shard_map/all_to_all | solution.py:194
  666.4 12.7 fusion
  680.2 57.5 %all_to_all.31 = bf16[16,1024,128]{2,1,0:T(8,128)(2,1)} all-to-all(bf16[16,1024,128]{2,1,0:T(8,128)(2,1)S(1)} %bitcast.38), channel_id=1, replica_groups=mesh['rep'=4,'z'=4,'y'=4,'core'=2] {'z','y'}, dimensions={0} | all-to-all | bytes 8388608 | tf_op jit(solution)/shard_map/all_to_all | solution.py:200
  737.8 153.7 %all-gather.17.cloned.1.call-done = bf16[128,1024,128]{2,1,0:T(8,128)(2,1)} async-done(((bf16[16,1024,128]{2,1,0:T(8,128)(2,1)}), bf16[128,1024,128]{2,1,0:T(8,128)(2,1)}) %all-gather.17.cloned.1.call-update) | async-done | bytes 33554448 | tf_op jit(solution)/shard_map/all_gather | solution.py:201
  891.5 372.3 %layer_two.1 = bf16[16384,128]{1,0:T(8,128)(2,1)} custom-call(s32[2]{0:T(128)} %pad_add_fusion.meta_ref, s32[524288]{0:T(1024)} %bitcast.46, bf16[640,8,128]{2,1,0:T(8,128)(2,1)} %bitcast.48, bf16[4,32,1024,128]{3,2,1,0:T(8,128)(2,1)} %bitcast.37), custom_call_target="tpu_custom_call" | custom-call | flops 1024000000 | bytes 33554432 | tf_op jit(solution)/shard_map/layer_two/pallas_call | solution.py:142
  1263.8 6.4 copy.31
  1270.2 59.0 %all_to_all.32 = bf16[16,1024,128]{1,2,0:T(8,128)(2,1)S(1)} all-to-all(bf16[16,1024,128]{1,2,0:T(8,128)(2,1)} %copy.31), channel_id=1, replica_groups=mesh['rep'=4,'z'=4,'y'=4,'core'=2] {'z','y'}, dimensions={0} | all-to-all | bytes 8388608 | tf_op jit(solution)/shard_map/all_to_all | solution.py:194
  1331.5 2.0 copy.23
  1336.8 49.1 %all-gather.19.cloned.1.call-done = bf16[32768,128]{1,0:T(8,128)(2,1)} async-done(((bf16[1024,128]{1,0:T(8,128)(2,1)}), bf16[32768,128]{1,0:T(8,128)(2,1)}) %all-gather.19.cloned.1.call-update) | async-done | bytes 8388624 | tf_op jit(solution)/shard_map/all_gather | solution.py:206
  1385.9 26.7 %layer_three.1 = f32[4096,128]{1,0:T(8,128)} custom-call(s32[2]{0:T(128)} %pad_add_fusion.meta_ref, s32[32768]{0:T(1024)} %reshape.167.idx_hbm, bf16[32,8,128]{2,1,0:T(8,128)(2,1)} %copy.32.wt_ref, bf16[1,32,1024,128]{3,2,1,0:T(8,128)(2,1)} %bitcast.43), custom_call_target="tpu_custom_call" | custom-call | flops 64000000 | bytes 33554432 | tf_op jit(solution)/shard_map/layer_three/pallas_call | solution.py:142
  1412.7 28.6 %reduce-scatter.2.cloned.1.call-done = f32[1024,128]{1,0:T(8,128)} async-done(((f32[4096,128]{1,0:T(8,128)}), f32[1024,128]{1,0:T(8,128)}) %reduce-scatter.2.cloned.1.call-update) | async-done | bytes 524304 | tf_op jit(solution)/shard_map/reduce_scatter | solution.py:209
  1441.3 2.0 fusion.2
  (52 shorter events, 18.4 us)
Async XLA Ops:
  6.5 32.4 %copy-start = (bf16[50,2048]{1,0:T(8,128)(2,1)S(1)}, bf16[50,2048]{1,0:T(8,128)(2,1)}, u32[]{:S(2)}) copy-start(bf16[50,2048]{1,0:T(8,128)(2,1)} %param.21) | copy-start | bytes 614404
  6.5 17.9 %copy-start.4 = (s32[4096,8]{0,1:T(8,128)S(1)}, s32[4096,8]{0,1:T(8,128)}, u32[]{:S(2)}) copy-start(s32[4096,8]{0,1:T(8,128)} %param.18) | copy-start | bytes 393220
  6.5 96.3 %all-gather.15.cloned.1.call-start = ((), (), s32[]{:S(2)}) async-start(), calls=%async_computation.9 | async-start | bytes 16908288 | tf_op jit(solution)/shard_map/all_gather | solution.py:175
  14.6 9.1 all-to-all-start.1
  19.5 126.0 %all-gather.13.cloned.1.call-start = ((), (), s32[]{:S(2)}) async-start(), calls=%async_computation.8 | async-start | bytes 1392640 | tf_op jit(solution)/shard_map/all_gather | solution.py:187
  24.4 167.8 %all-gather.11.cloned.1.call-start = ((), (), s32[]{:S(2)}) async-start(), calls=%async_computation.7 | async-start | bytes 2228224 | tf_op jit(solution)/shard_map/all_gather | solution.py:183
  39.4 85.7 %copy-start.3 = (bf16[128,256]{1,0:T(8,128)(2,1)}, bf16[128,256]{1,0:T(8,128)(2,1)S(1)}, u32[]{:S(2)}) copy-start(bf16[128,256]{1,0:T(8,128)(2,1)S(1)} %scatter.9.refs_0_) | copy-start | bytes 196612
  602.6 5.1 copy-start.5
  602.6 63.8 %all-to-all-start.2 = ((bf16[16,1024,128]{1,2,0:T(8,128)(2,1)}), bf16[16,1024,128]{1,2,0:T(8,128)(2,1)}, u32[]{:S(2)}, u32[]{:S(2)}) async-start(bf16[16,1024,128]{1,2,0:T(8,128)(2,1)} %copy.29), calls=%async_computation.2 | async-start | bytes 8388608 | tf_op jit(solution)/shard_map/all_to_all | solution.py:194
  607.5 284.0 %all-gather.17.cloned.1.call-start = ((), (), s32[]{:S(2)}) async-start(), calls=%async_computation.10 | async-start | bytes 37748736 | tf_op jit(solution)/shard_map/all_gather | solution.py:201
  737.8 648.2 %all-gather.19.cloned.1.call-start = ((), (), s32[]{:S(2)}) async-start(), calls=%async_computation.11 | async-start | bytes 8650752 | tf_op jit(solution)/shard_map/all_gather | solution.py:206
  1270.2 59.0 %copy-start.6 = (bf16[2048,121]{1,0:T(8,128)(2,1)S(1)}, bf16[2048,121]{1,0:T(8,128)(2,1)}, u32[]{:S(2)}) copy-start(bf16[2048,121]{1,0:T(8,128)(2,1)} %param.23) | copy-start | bytes 1486852
  1331.2 110.1 %reduce-scatter.2.cloned.1.call-start = ((), (), s32[]{:S(2)}) async-start(), calls=%async_computation.6 | async-start | bytes 2621440 | tf_op jit(solution)/shard_map/reduce_scatter | solution.py:209
  1385.9 55.4 %copy-start.2 = (bf16[1024,128]{1,0:T(8,128)(2,1)S(1)}, bf16[1024,128]{1,0:T(8,128)(2,1)}, u32[]{:S(2)}) copy-start(bf16[1024,128]{1,0:T(8,128)(2,1)} %fusion.1) | copy-start | bytes 786436
  1385.9 57.4 %copy-start.1 = (bf16[50,2048]{1,0:T(8,128)(2,1)S(1)}, bf16[50,2048]{1,0:T(8,128)(2,1)}, u32[]{:S(2)}) copy-start(bf16[50,2048]{1,0:T(8,128)(2,1)} %param.21) | copy-start | bytes 614404
Sparse Core Ops, SparseCore 0:
  10.2 92.5 all-gather.14
  104.9 40.4 all-gather.12
  147.6 44.5 all-gather.10
  737.9 153.5 all-gather.16
  1331.4 54.5 all-gather.18
  1412.8 28.4 reduce-scatter.1
